TPU v7x, 256 devices: a whole 4x4x8 slice. The times are simulated.
256 devices in a mesh: member: 16 (over x, y_hi, core), tensor: 16 (over z, y_lo).
Axes of the slice: x: 4, y: 4 (y_hi: 2, y_lo: 2; y = y_hi * 2 + y_lo), z: 8, core: 2. Of those that a mesh axis runs over, the one named last changes fastest.
Arguments:
- prompt_acts: bfloat16 [128, 5120], P(None, 'member'), may hold values from -6 to 6
- gate_weight: bfloat16 [5120, 13824], P('member', 'tensor'), may hold values from -0.078125 to 0.078125
- up_weight: bfloat16 [5120, 13824], P('member', 'tensor'), may hold values from -0.078125 to 0.078125
- down_weight: bfloat16 [13824, 5120], P('tensor', 'member'), may hold values from -0.0546875 to 0.0546875
- d_table: bfloat16 [256, 3, 4, 5120], P('member'), may hold values from -6 to 6
- f_table: bfloat16 [256, 3, 4, 13824], P('member', None, None, 'tensor'), may hold values from -6 to 6
- seeds: int32 [128], P('member'), may hold values from 0 to 15
- fitness: float32 [128], P('member'), may hold values from -6 to 6
Outputs:
- outputs: bfloat16 [128, 128, 5120], P('member', None, 'tensor')
- delta_gate: bfloat16 [5120, 13824], P('member', 'tensor')
- delta_up: bfloat16 [5120, 13824], P('member', 'tensor')
- delta_down: bfloat16 [13824, 5120], P('tensor', 'member')
Inputs may be any that keep to these rules, and one draw needn't show every extreme that they name: Member m uses row (m // 8) * 16 + seeds[m] of both tables, a row in its own group's block.
All inputs are finite; a program needn't handle non-finite values.
Results may differ from a plain program's by a relative error of at most 0.025.
Values may be sent and summed in bfloat16 or wider, within the bound.
A program may use at most 128 MiB of HBM per device.

v0:
```python
import math
import jax
import jax.numpy as jnp
from jax import lax
from jax.sharding import Mesh
from jax.sharding import PartitionSpec as P

D = 5120
FFW = 13824
MEMBER = ("member_0", "member_1", "member_2")
TENSOR = ("tensor_0", "tensor_1")
perturb_gain = 0.5


def sent_to_all(shard, axis):
    devices = lax.axis_size(axis)
    return lax.all_to_all(
        jnp.broadcast_to(shard[None], (devices, *shard.shape)), axis, 0, 0, tiled=True
    )


def joined_along(parts, dim):
    dims = list(parts.shape[1:])
    dims[dim] *= parts.shape[0]
    return jnp.moveaxis(parts, 0, dim).reshape(dims)


def gather_axes(shard, axes, dim):
    far, near = axes
    leading = sent_to_all(shard, far)
    parts = jnp.swapaxes(sent_to_all(leading, near), 0, 1)
    return joined_along(parts.reshape(-1, *shard.shape), dim)


def gather_directly(shard, axis, dim):
    return joined_along(sent_to_all(shard, axis), dim)


def filled_up(lines, devices):
    spare = -len(lines) % devices
    return jnp.pad(lines, [(0, spare)] + [(0, 0)] * (lines.ndim - 1))


def cut_along(shard, dim, devices):
    before, after = (shard.shape[:dim], shard.shape[dim + 1 :])
    return jnp.moveaxis(shard.reshape(*before, devices, -1, *after), dim, 0)


def sent_and_summed(shard, axis, dim):
    devices = lax.axis_size(axis)
    parts = lax.all_to_all(cut_along(shard, dim, devices), axis, 0, 0, tiled=True)
    return jnp.sum(parts.astype(jnp.float32), axis=0)


def sum_in_two_steps(shard, axes, dim):
    far, near = axes
    own = sent_and_summed(cut_along(shard, dim, lax.axis_size(far)), near, dim + 1)
    return jnp.sum(
        lax.all_to_all(own.astype(jnp.bfloat16), far, 0, 0, tiled=True).astype(jnp.float32), axis=0
    )


def sum_by_parts(shard, axes):
    lines = shard.reshape(-1, shard.shape[-1])
    padded = filled_up(lines, lax.axis_size(axes[0]) * lax.axis_size(axes[1]))
    whole = gather_axes(sum_in_two_steps(padded, axes, 0).astype(jnp.bfloat16), axes, 0)
    return lax.slice_in_dim(whole, 0, len(lines)).reshape(shard.shape).astype(jnp.float32)


def taken_together(shard, axis):
    return sent_to_all(shard, axis).sum(axis=0)


def scatter_axes(shard, axes, dim):
    if not axes:
        return shard
    nearer = lax.psum_scatter(shard, axes[0], scatter_dimension=dim, tiled=True)
    return scatter_axes(nearer, axes[1:], dim)


def shards(prompt_acts, gate_weight, up_weight, down_weight, d_table, f_table, seeds, fitness):
    members = seeds.shape[0]
    prompt_len = prompt_acts.shape[0]
    rank_size = d_table.shape[2]
    d_sel = jnp.take(d_table, seeds, axis=0)
    selected_factors = jnp.take(f_table, seeds, axis=0)
    d_slices = lax.all_to_all(d_sel, MEMBER, split_axis=3, concat_axis=0, tiled=True)
    f_all, fit_all = (
        gather_axes(selected_factors, (("member_0", "member_1"), "member_2"), 0),
        gather_axes(fitness.astype(jnp.bfloat16), (("member_0", "member_1"), "member_2"), 0).astype(
            fitness.dtype
        ),
    )
    population = fit_all.shape[0]
    gate_part = jnp.dot(prompt_acts, gate_weight, preferred_element_type=jnp.float32)
    up_part = jnp.dot(prompt_acts, up_weight, preferred_element_type=jnp.float32)
    prompt_full = gather_directly(prompt_acts, MEMBER, 1)
    gate_sum, up_sum = (
        sum_by_parts(gate_part.astype(jnp.bfloat16), (("member_0", "member_1"), "member_2")),
        sum_by_parts(up_part.astype(jnp.bfloat16), (("member_0", "member_1"), "member_2")),
    )
    in_factors = d_sel[:, :2].reshape(members * 2 * rank_size, D)
    proj_sum = jnp.dot(prompt_full, in_factors.T, preferred_element_type=jnp.float32)
    base_gate = gate_sum.astype(jnp.bfloat16)
    base_up = up_sum.astype(jnp.bfloat16)
    proj_inputs = (
        (proj_sum / math.sqrt(D)).astype(jnp.bfloat16).reshape(prompt_len, members, 2, rank_size)
    )
    perturbed = jnp.einsum(
        "pmkr,mkrf->mkpf", proj_inputs, selected_factors[:, :2], preferred_element_type=jnp.float32
    )
    gate = base_gate.astype(jnp.float32)[None] + perturb_gain * perturbed[:, 0]
    up = base_up.astype(jnp.float32)[None] + perturb_gain * perturbed[:, 1]
    hidden_state = (jax.nn.silu(gate) * up).astype(jnp.bfloat16)
    projection_here = jnp.einsum(
        "cdv,czv->cdz", hidden_state, selected_factors[:, 2], preferred_element_type=jnp.float32
    )
    proj_down = (taken_together(projection_here, TENSOR) / math.sqrt(FFW)).astype(jnp.bfloat16)
    hidden_rows = hidden_state.reshape(members * prompt_len, hidden_state.shape[2])
    partial_value = jnp.dot(
        hidden_rows,
        lax.all_gather(down_weight, MEMBER, axis=1, tiled=True),
        preferred_element_type=jnp.float32,
    )
    summed = scatter_axes(partial_value.astype(jnp.bfloat16), TENSOR, 1).astype(jnp.float32)
    local_column_range = summed.shape[1]
    col_start = lax.axis_index(TENSOR) * local_column_range
    out_factor = lax.dynamic_slice_in_dim(d_sel[:, 2], col_start, local_column_range, 2)
    down_noise_delta = perturb_gain * jnp.einsum(
        "mpr,mrd->mpd", proj_down, out_factor, preferred_element_type=jnp.float32
    )
    outputs = (summed.reshape(members, prompt_len, local_column_range) + down_noise_delta).astype(
        jnp.bfloat16
    )
    mean = jnp.sum(fit_all) / population
    spread = jnp.sum((fit_all - mean) ** 2) / population
    score = (fit_all - mean) / jnp.sqrt(spread + 1.0)
    weighted = (d_slices.astype(jnp.float32) * score[:, None, None, None]).astype(jnp.bfloat16)
    scale = 1.0 / math.sqrt(population * rank_size)
    width_cols = weighted.shape[3]
    hidden_cols = f_all.shape[3]
    w_gate = weighted[:, 0].reshape(population * rank_size, width_cols)
    w_up = weighted[:, 1].reshape(population * rank_size, width_cols)
    w_down = weighted[:, 2].reshape(population * rank_size, width_cols)
    f_gate = f_all[:, 0].reshape(population * rank_size, hidden_cols)
    f_up = f_all[:, 1].reshape(population * rank_size, hidden_cols)
    down_factor_columns = f_all[:, 2].reshape(population * rank_size, hidden_cols)
    delta_gate = (jnp.dot(w_gate.T, f_gate, preferred_element_type=jnp.float32) * scale).astype(
        jnp.bfloat16
    )
    delta_up = (jnp.dot(w_up.T, f_up, preferred_element_type=jnp.float32) * scale).astype(
        jnp.bfloat16
    )
    delta_down = (
        jnp.dot(down_factor_columns.T, w_down, preferred_element_type=jnp.float32) * scale
    ).astype(jnp.bfloat16)
    return (outputs, delta_gate, delta_up, delta_down)


def solution(mesh):
    split = Mesh(
        mesh.devices.reshape(4, 2, 2, 8, 2),
        ("member_0", "member_1", "member_2", "tensor_0", "tensor_1"),
    )
    placed = (
        P(None, MEMBER),
        P(MEMBER, TENSOR),
        P(MEMBER, TENSOR),
        P(TENSOR, MEMBER),
        P(MEMBER, None, None, None),
        P(MEMBER, None, None, TENSOR),
        P(MEMBER),
        P(MEMBER),
    )
    return jax.shard_map(
        shards,
        mesh=split,
        in_specs=placed,
        out_specs=(
            P(MEMBER, None, TENSOR),
            P(MEMBER, TENSOR),
            P(MEMBER, TENSOR),
            P(TENSOR, MEMBER),
        ),
        check_vma=False,
    )
```

profile of v0, /device:TPU:2, one launch (start us, length us, event | category | flops | bytes accessed | tf_op | source)
XLA Modules:
  0.0 367.8 jit_solution(5300602378496376444)
XLA Ops:
  10.3 3.4 all-to-all-start.5
  16.2 3.4 all-to-all-start
  21.2 7.5 %all-to-all-start.6 = ((bf16[8,8,864]{2,1,0:T(8,128)(2,1)}), bf16[8,8,864]{2,1,0:T(8,128)(2,1)S(1)}, u32[]{:S(2)}, u32[]{:S(2)}) async-start(bf16[8,8,864]{2,1,0:T(8,128)(2,1)} %reduce_sum.77), calls=%async_computation.6 | async-start | bytes 229376 | tf_op jit(solution)/shard_map/all_to_all | solution.py:59
  29.3 6.2 %all-to-all-done.6 = bf16[8,8,864]{2,1,0:T(8,128)(2,1)S(1)} async-done(((bf16[8,8,864]{2,1,0:T(8,128)(2,1)}), bf16[8,8,864]{2,1,0:T(8,128)(2,1)S(1)}, u32[]{:S(2)}, u32[]{:S(2)}) %all-to-all-start.6) | async-done | bytes 110624 | tf_op jit(solution)/shard_map/all_to_all | solution.py:59
  35.5 5.4 %all-to-all-start.1 = ((bf16[8,8,864]{2,1,0:T(8,128)(2,1)}), bf16[8,8,864]{2,1,0:T(8,128)(2,1)S(1)}, u32[]{:S(2)}, u32[]{:S(2)}) async-start(bf16[8,8,864]{2,1,0:T(8,128)(2,1)} %reduce_sum.75), calls=%async_computation.1 | async-start | bytes 229376 | tf_op jit(solution)/shard_map/all_to_all | solution.py:59
  40.9 6.3 %all-to-all-done.1 = bf16[8,8,864]{2,1,0:T(8,128)(2,1)S(1)} async-done(((bf16[8,8,864]{2,1,0:T(8,128)(2,1)}), bf16[8,8,864]{2,1,0:T(8,128)(2,1)S(1)}, u32[]{:S(2)}, u32[]{:S(2)}) %all-to-all-start.1) | async-done | bytes 110624 | tf_op jit(solution)/shard_map/all_to_all | solution.py:59
  47.9 4.8 %all-to-all-start.7 = ((bf16[8,8,864]{2,1,0:T(8,128)(2,1)}), bf16[8,8,864]{2,1,0:T(8,128)(2,1)S(1)}, u32[]{:S(2)}, u32[]{:S(2)}) async-start(bf16[8,8,864]{2,1,0:T(8,128)(2,1)} %broadcast_in_dim.52), calls=%async_computation.7 | async-start | bytes 229376 | tf_op jit(solution)/shard_map/all_to_all | solution.py:17
  52.7 6.4 %all-to-all-done.7 = bf16[8,8,864]{2,1,0:T(8,128)(2,1)S(1)} async-done(((bf16[8,8,864]{2,1,0:T(8,128)(2,1)}), bf16[8,8,864]{2,1,0:T(8,128)(2,1)S(1)}, u32[]{:S(2)}, u32[]{:S(2)}) %all-to-all-start.7) | async-done | bytes 110624 | tf_op jit(solution)/shard_map/all_to_all | solution.py:17
  59.1 3.9 %all_to_all.80 = bf16[2,8,8,864]{3,2,1,0:T(8,128)(2,1)S(1)} all-to-all(bf16[2,8,8,864]{3,2,1,0:T(8,128)(2,1)S(1)} %broadcast_in_dim.53), channel_id=1, replica_groups=mesh['member_0'=4,'member_1'=2,'member_2'=2,'tensor_0'=8,'tensor_1'=2] {..., dimensions={0} | all-to-all | bytes 442368 | tf_op jit(solution)/shard_map/all_to_all | solution.py:17
  63.6 4.9 %all-to-all-start.2 = ((bf16[8,8,864]{2,1,0:T(8,128)(2,1)}), bf16[8,8,864]{2,1,0:T(8,128)(2,1)S(1)}, u32[]{:S(2)}, u32[]{:S(2)}) async-start(bf16[8,8,864]{2,1,0:T(8,128)(2,1)} %broadcast_in_dim.44), calls=%async_computation.2 | async-start | bytes 229376 | tf_op jit(solution)/shard_map/all_to_all | solution.py:17
  70.8 4.4 %all-to-all-done.2 = bf16[8,8,864]{2,1,0:T(8,128)(2,1)S(1)} async-done(((bf16[8,8,864]{2,1,0:T(8,128)(2,1)}), bf16[8,8,864]{2,1,0:T(8,128)(2,1)S(1)}, u32[]{:S(2)}, u32[]{:S(2)}) %all-to-all-start.2) | async-done | bytes 110624 | tf_op jit(solution)/shard_map/all_to_all | solution.py:17
  75.2 4.6 %all_to_all.81 = bf16[2,8,8,864]{3,2,1,0:T(8,128)(2,1)} all-to-all(bf16[2,8,8,864]{3,2,1,0:T(8,128)(2,1)S(1)} %broadcast_in_dim.45), channel_id=1, replica_groups=mesh['member_0'=4,'member_1'=2,'member_2'=2,'tensor_0'=8,'tensor_1'=2] {..., dimensions={0} | all-to-all | bytes 442368 | tf_op jit(solution)/shard_map/all_to_all | solution.py:17
  81.1 5.3 %all-to-all-start.4 = ((bf16[16,128,320]{1,2,0:T(8,128)(2,1)}), bf16[16,128,320]{1,2,0:T(8,128)(2,1)S(1)}, u32[]{:S(2)}, u32[]{:S(2)}) async-start(bf16[16,128,320]{1,2,0:T(8,128)(2,1)} %broadcast_in_dim.49), calls=%async_computation.4 | async-start | bytes 2621440 | tf_op jit(solution)/shard_map/all_to_all | solution.py:17
  95.5 12.5 %all-to-all-done.4 = bf16[16,128,320]{1,2,0:T(8,128)(2,1)S(1)} async-done(((bf16[16,128,320]{1,2,0:T(8,128)(2,1)}), bf16[16,128,320]{1,2,0:T(8,128)(2,1)S(1)}, u32[]{:S(2)}, u32[]{:S(2)}) %all-to-all-start.4) | async-done | bytes 1310752 | tf_op jit(solution)/shard_map/all_to_all | solution.py:17
  110.8 3.8 %copy.156 = f32[8,1,128,864]{2,0,3,1:T(8,128)} copy(f32[8,1,128,864]{2,3,1,0:T(8,128)S(1)} %slice_multiply_fusion) | data formatting | bytes 7077888 | tf_op jit(solution)/shard_map/mul | solution.py:113
  114.9 3.8 %copy.149 = f32[8,1,128,864]{2,0,3,1:T(8,128)} copy(f32[8,1,128,864]{2,3,0,1:T(8,128)S(1)} %fusion.2) | data formatting | bytes 7077888 | tf_op jit(solution)/shard_map/mul | solution.py:112
  122.8 25.7 %convolution_convert_fusion = bf16[1024,5120]{1,0:T(8,128)(2,1)} fusion(bf16[864,5120]{0,1:T(8,128)(2,1)} %all-gather.2.cloned.1.call-done, f32[108,8,8,128]{3,2,1,0:T(8,128)} %bitcast.163, f32[108,8,8,128]{3,2,1,0:T(8,128)} %bitcast.165, f32[108,8,8,128]{3,2,1,0:T(8,128)} %bitcast.164, f32[108,8,8,128]{3,2,1,0:T(8,128)} %bitcast.166), kind=kOutput, calls=%fused_computation.2 | convolution fusion | flops 9072017408 | bytes 33488896 | tf_op jit(solution)/shard_map/dot_general | solution.py:120
  148.5 14.4 %copy.171 = bf16[1024,5120]{0,1:T(8,128)(2,1)} copy(bf16[1024,5120]{1,0:T(8,128)(2,1)} %convolution_convert_fusion) | data formatting | bytes 20971520
  164.1 8.8 %all-to-all-start.11 = ((bf16[8,1,8]{2,1,0:T(2,128)(2,1)}), bf16[8,1,8]{2,1,0:T(2,128)(2,1)S(1)}, u32[]{:S(2)}, u32[]{:S(2)}) async-start(bf16[8,1,8]{2,1,0:T(2,128)(2,1)} %broadcast_in_dim.98), calls=%async_computation.11 | async-start | bytes 8192 | tf_op jit(solution)/shard_map/all_to_all | solution.py:17
  172.9 15.0 %copy.161 = bf16[8,3,4,5120]{0,2,1,3:T(4,128)(2,1)} copy(bf16[8,3,4,5120]{3,2,1,0:T(4,128)(2,1)S(1)} %broadcast_select_fusion) | data formatting | bytes 1966080 | tf_op jit(solution)/shard_map/jit(_take)/select_n | solution.py:85
  188.0 20.0 %reshape.151 = bf16[16,2,15360]{2,1,0:T(2,128)(2,1)} reshape(bf16[5120,3,4,8]{3,2,1,0:T(4,128)(2,1)} %bitcast.156) | data formatting | bytes 1966080
  208.0 3.7 %all_to_all.82 = bf16[2,8,8]{2,1,0:T(8,128)(2,1)S(1)} all-to-all(bf16[2,8,8]{2,1,0:T(8,128)(2,1)S(1)} %broadcast_in_dim.100), channel_id=1, replica_groups=mesh['member_0'=4,'member_1'=2,'member_2'=2,'tensor_0'=8,'tensor_1'=2] {..., dimensions={0} | all-to-all | bytes 512 | tf_op jit(solution)/shard_map/all_to_all | solution.py:17
  211.7 7.2 %all-to-all-start.10 = ((bf16[16,2,15360]{2,1,0:T(2,128)(2,1)}), bf16[16,2,15360]{2,1,0:T(2,128)(2,1)S(1)}, u32[]{:S(2)}, u32[]{:S(2)}) async-start(bf16[16,2,15360]{2,1,0:T(2,128)(2,1)} %reshape.151), calls=%async_computation.10 | async-start | bytes 1966080 | tf_op jit(solution)/shard_map/all_to_all | solution.py:87
  218.9 15.0 %all-to-all-done.10 = bf16[16,2,15360]{2,1,0:T(2,128)(2,1)S(1)} async-done(((bf16[16,2,15360]{2,1,0:T(2,128)(2,1)}), bf16[16,2,15360]{2,1,0:T(2,128)(2,1)S(1)}, u32[]{:S(2)}, u32[]{:S(2)}) %all-to-all-start.10) | async-done | bytes 983072 | tf_op jit(solution)/shard_map/all_to_all | solution.py:87
  235.2 6.4 %all-to-all-start.13 = ((bf16[8,8,3,4,864]{4,1,3,2,0:T(8,128)(2,1)}), bf16[8,8,3,4,864]{4,1,3,2,0:T(8,128)(2,1)}, u32[]{:S(2)}, u32[]{:S(2)}) async-start(bf16[8,8,3,4,864]{4,1,3,2,0:T(8,128)(2,1)} %broadcast_in_dim.101), calls=%async_computation.13 | async-start | bytes 2752512 | tf_op jit(solution)/shard_map/all_to_all | solution.py:17
  241.6 39.1 %reduce-scatter.7.cloned.1.call-done = bf16[640,1024]{1,0:T(8,128)(2,1)} async-done(((bf16[5120,1024]{1,0:T(8,128)(2,1)}), bf16[640,1024]{1,0:T(8,128)(2,1)}) %reduce-scatter.7.cloned.1.call-update) | async-done | bytes 1310736
  283.5 19.3 %reshape.152 = bf16[5120,3,4,8]{3,2,1,0:T(4,128)(2,1)} reshape(bf16[16,2,15360]{2,1,0:T(2,128)(2,1)S(1)} %all-to-all-done.10) | data formatting | bytes 1966080
  302.8 21.0 %copy.162 = f32[8,3,4,16,320]{4,0,3,2,1:T(8,128)} copy(bf16[8,3,4,16,320]{0,2,1,4,3:T(4,128)(2,1)} %bitcast.155) | data formatting | bytes 2949120 | tf_op jit(solution)/shard_map/convert_element_type | solution.py:138
  328.4 6.2 %all_to_all.83 = bf16[2,8,8,3,4,864]{5,2,1,4,3,0:T(8,128)(2,1)S(1)} all-to-all(bf16[2,8,8,3,4,864]{5,2,1,4,3,0:T(8,128)(2,1)S(1)} %broadcast_in_dim.102), channel_id=1, replica_groups=mesh['member_0'=4,'member_1'=2,'member_2'=2,'tensor_0'=8,'tensor_1'=2] {..., dimensions={0} | all-to-all | bytes 5308416 | tf_op jit(solution)/shard_map/all_to_all | solution.py:17
  340.7 5.5 %all-to-all-start.9 = ((f32[16,8,128,4]{2,1,3,0:T(8,128)}), f32[16,8,128,4]{2,1,3,0:T(8,128)S(1)}, u32[]{:S(2)}, u32[]{:S(2)}) async-start(f32[16,8,128,4]{2,1,3,0:T(8,128)} %broadcast_in_dim.54), calls=%async_computation.9 | async-start | bytes 524288 | tf_op jit(solution)/shard_map/all_to_all | solution.py:17
  346.3 2.6 fusion.15
  351.5 7.2 %all-to-all-done.9 = f32[16,8,128,4]{2,1,3,0:T(8,128)S(1)} async-done(((f32[16,8,128,4]{2,1,3,0:T(8,128)}), f32[16,8,128,4]{2,1,3,0:T(8,128)S(1)}, u32[]{:S(2)}, u32[]{:S(2)}) %all-to-all-start.9) | async-done | bytes 262176 | tf_op jit(solution)/shard_map/all_to_all | solution.py:17
  (107 shorter events, 48.6 us)
Async XLA Ops:
  7.2 61.3 %copy-start = (bf16[16,3,4,5120]{3,2,1,0:T(4,128)(2,1)S(1)}, bf16[16,3,4,5120]{3,2,1,0:T(4,128)(2,1)}, u32[]{:S(2)}) copy-start(bf16[16,3,4,5120]{3,2,1,0:T(4,128)(2,1)} %param.12) | copy-start | bytes 5898244
  7.2 33.7 %copy-start.12 = (s32[8]{0:T(128)S(1)}, s32[8]{0:T(128)}, u32[]{:S(2)}) copy-start(s32[8]{0:T(128)} %param.14) | copy-start | bytes 100
  7.2 111.5 %all-gather.2.cloned.1.call-start = ((), (), s32[]{:S(2)}) async-start(), calls=%async_computation.17 | async-start | bytes 9748480 | tf_op jit(solution)/shard_map/all_gather | solution.py:122
  10.3 5.9 %all-to-all-start.5 = ((bf16[2,8,8,864]{3,2,1,0:T(8,128)(2,1)}), bf16[2,8,8,864]{3,2,1,0:T(8,128)(2,1)S(1)}, u32[]{:S(2)}, u32[]{:S(2)}) async-start(bf16[2,8,8,864]{3,2,1,0:T(8,128)(2,1)} %copy.151), calls=%async_computation.5 | async-start | bytes 458752 | tf_op jit(solution)/shard_map/all_to_all | solution.py:51
  15.3 64.5 %copy-start.10 = (bf16[128,320]{0,1:T(8,128)(2,1)S(1)}, bf16[128,320]{0,1:T(8,128)(2,1)}, u32[]{:S(2)}) copy-start(bf16[128,320]{0,1:T(8,128)(2,1)} %param.8) | copy-start | bytes 245764
  16.2 5.0 %all-to-all-start = ((bf16[2,8,8,864]{3,2,1,0:T(8,128)(2,1)}), bf16[2,8,8,864]{3,2,1,0:T(8,128)(2,1)S(1)}, u32[]{:S(2)}, u32[]{:S(2)}) async-start(bf16[2,8,8,864]{3,2,1,0:T(8,128)(2,1)} %copy.144), calls=%async_computation | async-start | bytes 458752 | tf_op jit(solution)/shard_map/all_to_all | solution.py:51
  21.2 14.3 %all-to-all-start.6 = ((bf16[8,8,864]{2,1,0:T(8,128)(2,1)}), bf16[8,8,864]{2,1,0:T(8,128)(2,1)S(1)}, u32[]{:S(2)}, u32[]{:S(2)}) async-start(bf16[8,8,864]{2,1,0:T(8,128)(2,1)} %reduce_sum.77), calls=%async_computation.6 | async-start | bytes 229376 | tf_op jit(solution)/shard_map/all_to_all | solution.py:59
  35.5 11.7 %all-to-all-start.1 = ((bf16[8,8,864]{2,1,0:T(8,128)(2,1)}), bf16[8,8,864]{2,1,0:T(8,128)(2,1)S(1)}, u32[]{:S(2)}, u32[]{:S(2)}) async-start(bf16[8,8,864]{2,1,0:T(8,128)(2,1)} %reduce_sum.75), calls=%async_computation.1 | async-start | bytes 229376 | tf_op jit(solution)/shard_map/all_to_all | solution.py:59
  47.9 11.2 %all-to-all-start.7 = ((bf16[8,8,864]{2,1,0:T(8,128)(2,1)}), bf16[8,8,864]{2,1,0:T(8,128)(2,1)S(1)}, u32[]{:S(2)}, u32[]{:S(2)}) async-start(bf16[8,8,864]{2,1,0:T(8,128)(2,1)} %broadcast_in_dim.52), calls=%async_computation.7 | async-start | bytes 229376 | tf_op jit(solution)/shard_map/all_to_all | solution.py:17
  63.6 11.6 %all-to-all-start.2 = ((bf16[8,8,864]{2,1,0:T(8,128)(2,1)}), bf16[8,8,864]{2,1,0:T(8,128)(2,1)S(1)}, u32[]{:S(2)}, u32[]{:S(2)}) async-start(bf16[8,8,864]{2,1,0:T(8,128)(2,1)} %broadcast_in_dim.44), calls=%async_computation.2 | async-start | bytes 229376 | tf_op jit(solution)/shard_map/all_to_all | solution.py:17
  70.8 17.6 %copy-start.11 = (bf16[16,3,4,864]{3,2,1,0:T(4,128)(2,1)S(1)}, bf16[16,3,4,864]{3,2,1,0:T(4,128)(2,1)}, u32[]{:S(2)}) copy-start(bf16[16,3,4,864]{3,2,1,0:T(4,128)(2,1)} %param.13) | copy-start | bytes 995332
  81.1 26.9 %all-to-all-start.4 = ((bf16[16,128,320]{1,2,0:T(8,128)(2,1)}), bf16[16,128,320]{1,2,0:T(8,128)(2,1)S(1)}, u32[]{:S(2)}, u32[]{:S(2)}) async-start(bf16[16,128,320]{1,2,0:T(8,128)(2,1)} %broadcast_in_dim.49), calls=%async_computation.4 | async-start | bytes 2621440 | tf_op jit(solution)/shard_map/all_to_all | solution.py:17
  86.4 194.3 %reduce-scatter.7.cloned.1.call-start = ((), (), s32[]{:S(2)}) async-start(), calls=%async_computation.18 | async-start | bytes 11796480
  88.4 192.4 %copy-start.3 = (bf16[8,3,4,5120]{3,2,1,0:T(4,128)(2,1)}, bf16[8,3,4,5120]{3,2,1,0:T(4,128)(2,1)S(1)}, u32[]{:S(2)}) copy-start(bf16[8,3,4,5120]{3,2,1,0:T(4,128)(2,1)S(1)} %broadcast_select_fusion) | copy-start | bytes 2949124
  110.5 4.1 %copy-start.2 = (f32[8,2,128,864]{2,3,1,0:T(8,128)}, f32[8,2,128,864]{2,3,1,0:T(8,128)S(1)}, u32[]{:S(2)}) copy-start(f32[8,2,128,864]{2,3,1,0:T(8,128)S(1)} %fusion.18) | copy-start | bytes 21233668
  114.9 3.8 %copy-start.5 = (f32[128,864]{0,1:T(8,128)S(1)}, f32[128,864]{0,1:T(8,128)}, u32[]{:S(2)}) copy-start(f32[128,864]{0,1:T(8,128)} %copy.181) | copy-start | bytes 1327108
  118.7 2.1 copy-start.6
  162.9 0.7 copy-start.13
  164.1 43.8 %all-to-all-start.11 = ((bf16[8,1,8]{2,1,0:T(2,128)(2,1)}), bf16[8,1,8]{2,1,0:T(2,128)(2,1)S(1)}, u32[]{:S(2)}, u32[]{:S(2)}) async-start(bf16[8,1,8]{2,1,0:T(2,128)(2,1)} %broadcast_in_dim.98), calls=%async_computation.11 | async-start | bytes 8192 | tf_op jit(solution)/shard_map/all_to_all | solution.py:17
  188.0 30.9 %copy-start.8 = (bf16[8,3,4,864]{3,2,1,0:T(4,128)(2,1)S(1)}, bf16[8,3,4,864]{3,2,1,0:T(4,128)(2,1)}, u32[]{:S(2)}) copy-start(bf16[8,3,4,864]{3,2,1,0:T(4,128)(2,1)} %broadcast_select_fusion.1) | copy-start | bytes 497668
  211.7 22.3 %all-to-all-start.10 = ((bf16[16,2,15360]{2,1,0:T(2,128)(2,1)}), bf16[16,2,15360]{2,1,0:T(2,128)(2,1)S(1)}, u32[]{:S(2)}, u32[]{:S(2)}) async-start(bf16[16,2,15360]{2,1,0:T(2,128)(2,1)} %reshape.151), calls=%async_computation.10 | async-start | bytes 1966080 | tf_op jit(solution)/shard_map/all_to_all | solution.py:87
  235.2 90.9 %all-to-all-start.13 = ((bf16[8,8,3,4,864]{4,1,3,2,0:T(8,128)(2,1)}), bf16[8,8,3,4,864]{4,1,3,2,0:T(8,128)(2,1)}, u32[]{:S(2)}, u32[]{:S(2)}) async-start(bf16[8,8,3,4,864]{4,1,3,2,0:T(8,128)(2,1)} %broadcast_in_dim.101), calls=%async_computation.13 | async-start | bytes 2752512 | tf_op jit(solution)/shard_map/all_to_all | solution.py:17
  241.6 117.1 %reduce-scatter.9.cloned.1.call-start = ((), (), s32[]{:S(2)}) async-start(), calls=%async_computation.19 | async-start | bytes 1966080
  326.0 8.8 %copy-start.9 = (bf16[128,3,4,320]{0,3,2,1:T(8,128)(2,1)}, bf16[128,3,4,320]{0,3,2,1:T(8,128)(2,1)S(1)}, u32[]{:S(2)}) copy-start(bf16[128,3,4,320]{0,3,2,1:T(8,128)(2,1)S(1)} %multiply_convert_fusion) | copy-start | bytes 2949124
  328.4 7.8 %slice-start = ((s8[7077888]{0:T(1024)(128)(4,1)}), s8[4194304]{0:T(1024)(128)(4,1)S(1)}, s32[]{:S(2)}) async-start(s8[7077888]{0:T(1024)(128)(4,1)} %bitcast.158), calls=%async_computation.20 | async-start | bytes 8388608
  334.6 3.0 slice-start.1
  334.6 3.1 copy-start.7
  334.8 5.1 %copy-start.4 = (bf16[8,2,8,3,4,864]{5,2,1,0,4,3:T(8,128)(2,1)}, bf16[8,2,8,3,4,864]{5,2,1,0,4,3:T(8,128)(2,1)S(1)}, u32[]{:S(2)}) copy-start(bf16[8,2,8,3,4,864]{5,2,1,0,4,3:T(8,128)(2,1)S(1)} %copy.167) | copy-start | bytes 7962628
  340.0 18.8 %slice-start.2 = ((bf16[8,3,4,5120]{3,2,1,0:T(4,128)(2,1)}), bf16[8,1,4,5120]{3,2,1,0:T(4,128)(2,1)S(1)}, s32[]{:S(2)}) async-start(bf16[8,3,4,5120]{3,2,1,0:T(4,128)(2,1)} %copy-done.3), calls=%async_computation.22 | async-start | bytes 655360 | tf_op jit(solution)/shard_map/slice | solution.py:128
  340.0 21.3 %copy-start.1 = (bf16[16,3,4,5120]{3,2,1,0:T(4,128)(2,1)S(1)}, bf16[16,3,4,5120]{3,2,1,0:T(4,128)(2,1)}, u32[]{:S(2)}) copy-start(bf16[16,3,4,5120]{3,2,1,0:T(4,128)(2,1)} %param.12) | copy-start | bytes 5898244
  340.7 17.9 %all-to-all-start.9 = ((f32[16,8,128,4]{2,1,3,0:T(8,128)}), f32[16,8,128,4]{2,1,3,0:T(8,128)S(1)}, u32[]{:S(2)}, u32[]{:S(2)}) async-start(f32[16,8,128,4]{2,1,3,0:T(8,128)} %broadcast_in_dim.54), calls=%async_computation.9 | async-start | bytes 524288 | tf_op jit(solution)/shard_map/all_to_all | solution.py:17
Sparse Core Ops, SparseCore 0:
  10.7 98.1 all-gather.1
  163.0 117.7 reduce-scatter.6
  283.3 26.9 reduce-scatter.8
where the time goes:
time: 371 us; the launch traced here: 368 us
  local copies, waits for them, and re-layouts  123 us (33%)
  waiting for transfers between devices  98.7 us (27%)
  starting transfers between devices  62.9 us (17%)
  matrix products  42.5 us (11%)
  blocking collectives  18.4 us (5%)
  between operations  15.5 us (4%)
  other arithmetic  6.97 us (2%)
    unnamed x38, local copies, waits for them, and re-layouts  57.7 us
    unnamed x5, waiting for transfers between devices  39.9 us
    all_to_all x6, starting transfers between devices, sent_to_all(): lax.all_to_all(jnp.broadcast_to(shard[None], (devices, *shard.shape)), ax...  35.7 us
    all_to_all x6, waiting for transfers between devices, sent_to_all(): lax.all_to_all(jnp.broadcast_to(shard[None], (devices, *shard.shape)), ax...  30.5 us
    dot_general x1, matrix products, shards(): jnp.dot(hidden_rows, lax.all_gather(down_weight, MEMBER, axis=1, tiled=Tr...  25.7 us
    convert_element_type x2, local copies, waits for them, and re-layouts, shards(): d_slices.astype(jnp.float32) * score[:, None, None, None]  23.1 us
    all_to_all x4, blocking collectives, sent_to_all(): lax.all_to_all(jnp.broadcast_to(shard[None], (devices, *shard.shape)), ax...  18.4 us
    all_to_all x1, waiting for transfers between devices, shards(): lax.all_to_all(d_sel, MEMBER, split_axis=3, concat_axis=0, tiled=True)  15 us
  transfers between devices with their start and end apart: 14, of which 9 were waited for; matrix products, arithmetic and copies ran while one was open for 34% of the time, Pallas kernels for 0%

commit v1 on v0

--- a/solution.py
+++ b/solution.py
@@ -84,7 +84,10 @@
     rank_size = d_table.shape[2]
     d_sel = jnp.take(d_table, seeds, axis=0)
     selected_factors = jnp.take(f_table, seeds, axis=0)
-    d_slices = lax.all_to_all(d_sel, MEMBER, split_axis=3, concat_axis=0, tiled=True)
+    d_slices = jnp.concatenate(
+        lax.all_to_all(jnp.stack(jnp.split(d_sel, lax.axis_size(MEMBER), axis=3)), MEMBER, 0, 0),
+        axis=0,
+    )
     f_all, fit_all = (
         gather_axes(selected_factors, (("member_0", "member_1"), "member_2"), 0),
         gather_axes(fitness.astype(jnp.bfloat16), (("member_0", "member_1"), "member_2"), 0).astype(

time: 371 us -> 326 us (0.88)
  local copies, waits for them, and re-layouts: 123 us -> 53.5 us
  waiting for transfers between devices: 98.7 us -> 128 us
    unnamed x38 -> x61, local copies, waits for them, and re-layouts: 57.7 us -> 22.1 us
    unnamed x5, waiting for transfers between devices: 39.9 us -> 66.6 us
    convert_element_type x2 -> x1, local copies, waits for them, and re-layouts: 23.1 us -> 2.03 us  [shards(): d_slices.astype(jnp.float32) * score[:, None, None, None]]
    select_n x1 -> x0, local copies, waits for them, and re-layouts: 15 us -> none  [shards(): d_sel = jnp.take(d_table, seeds, axis=0)]
  transfers between devices with their start and end apart: 14 -> 14, of which waited for: 9 -> 11; matrix products, arithmetic and copies ran while one was open for 34% -> 16% of each run, Pallas kernels for 0% -> 0%
where the time goes in v1:
time: 326 us; the launch traced here: 324 us
  waiting for transfers between devices  128 us (39%)
  starting transfers between devices  59.7 us (18%)
  local copies, waits for them, and re-layouts  53.5 us (16%)
  matrix products  39.5 us (12%)
  blocking collectives  19.2 us (6%)
  between operations  15.6 us (5%)
  other arithmetic  8.47 us (3%)
    unnamed x5, waiting for transfers between devices  66.6 us
    all_to_all x6, starting transfers between devices, sent_to_all(): lax.all_to_all(jnp.broadcast_to(shard[None], (devices, *shard.shape)), ax...  34.8 us
    all_to_all x6, waiting for transfers between devices, sent_to_all(): lax.all_to_all(jnp.broadcast_to(shard[None], (devices, *shard.shape)), ax...  30.8 us
    dot_general x1, matrix products, shards(): jnp.dot(hidden_rows, lax.all_gather(down_weight, MEMBER, axis=1, tiled=Tr...  25.7 us
    unnamed x61, local copies, waits for them, and re-layouts  22.1 us
    all_to_all x4, blocking collectives, sent_to_all(): lax.all_to_all(jnp.broadcast_to(shard[None], (devices, *shard.shape)), ax...  19.2 us
    all_to_all x1, waiting for transfers between devices, shards(): lax.all_to_all(jnp.stack(jnp.split(d_sel, lax.axis_size(MEMBER), axis=3))...  17.2 us
    all_to_all x2, starting transfers between devices, sum_in_two_steps(): lax.all_to_all(own.astype(jnp.bfloat16), far, 0, 0, tiled=True)  12.6 us
  transfers between devices with their start and end apart: 14, of which 11 were waited for; matrix products, arithmetic and copies ran while one was open for 16% of the time, Pallas kernels for 0%

profile of v1, /device:TPU:2, one launch (start us, length us, event | category | flops | bytes accessed | tf_op | source)
XLA Modules:
  0.0 324.1 jit_solution(8344559745957618734)
XLA Ops:
  10.4 3.6 %all-to-all-start.5 = ((bf16[2,8,8,864]{3,2,1,0:T(8,128)(2,1)}), bf16[2,8,8,864]{3,2,1,0:T(8,128)(2,1)S(1)}, u32[]{:S(2)}, u32[]{:S(2)}) async-start(bf16[2,8,8,864]{3,2,1,0:T(8,128)(2,1)} %copy.176), calls=%async_computation.5 | async-start | bytes 458752 | tf_op jit(solution)/shard_map/all_to_all | solution.py:51
  15.5 3.4 %all-to-all-start = ((bf16[2,8,8,864]{3,2,1,0:T(8,128)(2,1)}), bf16[2,8,8,864]{3,2,1,0:T(8,128)(2,1)S(1)}, u32[]{:S(2)}, u32[]{:S(2)}) async-start(bf16[2,8,8,864]{3,2,1,0:T(8,128)(2,1)} %copy.167), calls=%async_computation | async-start | bytes 458752 | tf_op jit(solution)/shard_map/all_to_all | solution.py:51
  20.4 7.5 %all-to-all-start.6 = ((bf16[8,8,864]{2,1,0:T(8,128)(2,1)}), bf16[8,8,864]{2,1,0:T(8,128)(2,1)S(1)}, u32[]{:S(2)}, u32[]{:S(2)}) async-start(bf16[8,8,864]{2,1,0:T(8,128)(2,1)} %reduce_sum.77), calls=%async_computation.6 | async-start | bytes 229376 | tf_op jit(solution)/shard_map/all_to_all | solution.py:59
  28.6 6.3 %all-to-all-done.6 = bf16[8,8,864]{2,1,0:T(8,128)(2,1)S(1)} async-done(((bf16[8,8,864]{2,1,0:T(8,128)(2,1)}), bf16[8,8,864]{2,1,0:T(8,128)(2,1)S(1)}, u32[]{:S(2)}, u32[]{:S(2)}) %all-to-all-start.6) | async-done | bytes 110624 | tf_op jit(solution)/shard_map/all_to_all | solution.py:59
  34.9 5.2 %all-to-all-start.1 = ((bf16[8,8,864]{2,1,0:T(8,128)(2,1)}), bf16[8,8,864]{2,1,0:T(8,128)(2,1)S(1)}, u32[]{:S(2)}, u32[]{:S(2)}) async-start(bf16[8,8,864]{2,1,0:T(8,128)(2,1)} %reduce_sum.75), calls=%async_computation.1 | async-start | bytes 229376 | tf_op jit(solution)/shard_map/all_to_all | solution.py:59
  40.1 6.3 %all-to-all-done.1 = bf16[8,8,864]{2,1,0:T(8,128)(2,1)S(1)} async-done(((bf16[8,8,864]{2,1,0:T(8,128)(2,1)}), bf16[8,8,864]{2,1,0:T(8,128)(2,1)S(1)}, u32[]{:S(2)}, u32[]{:S(2)}) %all-to-all-start.1) | async-done | bytes 110624 | tf_op jit(solution)/shard_map/all_to_all | solution.py:59
  47.1 5.1 %all-to-all-start.7 = ((bf16[8,8,864]{2,1,0:T(8,128)(2,1)}), bf16[8,8,864]{2,1,0:T(8,128)(2,1)S(1)}, u32[]{:S(2)}, u32[]{:S(2)}) async-start(bf16[8,8,864]{2,1,0:T(8,128)(2,1)} %broadcast_in_dim.52), calls=%async_computation.7 | async-start | bytes 229376 | tf_op jit(solution)/shard_map/all_to_all | solution.py:17
  52.2 6.3 %all-to-all-done.7 = bf16[8,8,864]{2,1,0:T(8,128)(2,1)S(1)} async-done(((bf16[8,8,864]{2,1,0:T(8,128)(2,1)}), bf16[8,8,864]{2,1,0:T(8,128)(2,1)S(1)}, u32[]{:S(2)}, u32[]{:S(2)}) %all-to-all-start.7) | async-done | bytes 110624 | tf_op jit(solution)/shard_map/all_to_all | solution.py:17
  58.6 4.6 %all_to_all.76 = bf16[2,8,8,864]{3,2,1,0:T(8,128)(2,1)} all-to-all(bf16[2,8,8,864]{3,2,1,0:T(8,128)(2,1)S(1)} %broadcast_in_dim.53), channel_id=1, replica_groups=mesh['member_0'=4,'member_1'=2,'member_2'=2,'tensor_0'=8,'tensor_1'=2] {..., dimensions={0} | all-to-all | bytes 442368 | tf_op jit(solution)/shard_map/all_to_all | solution.py:17
  63.8 4.8 %all-to-all-start.2 = ((bf16[8,8,864]{2,1,0:T(8,128)(2,1)}), bf16[8,8,864]{2,1,0:T(8,128)(2,1)S(1)}, u32[]{:S(2)}, u32[]{:S(2)}) async-start(bf16[8,8,864]{2,1,0:T(8,128)(2,1)} %broadcast_in_dim.44), calls=%async_computation.2 | async-start | bytes 229376 | tf_op jit(solution)/shard_map/all_to_all | solution.py:17
  71.0 4.4 %all-to-all-done.2 = bf16[8,8,864]{2,1,0:T(8,128)(2,1)S(1)} async-done(((bf16[8,8,864]{2,1,0:T(8,128)(2,1)}), bf16[8,8,864]{2,1,0:T(8,128)(2,1)S(1)}, u32[]{:S(2)}, u32[]{:S(2)}) %all-to-all-start.2) | async-done | bytes 110624 | tf_op jit(solution)/shard_map/all_to_all | solution.py:17
  75.4 4.6 %all_to_all.77 = bf16[2,8,8,864]{3,2,1,0:T(8,128)(2,1)} all-to-all(bf16[2,8,8,864]{3,2,1,0:T(8,128)(2,1)S(1)} %broadcast_in_dim.45), channel_id=1, replica_groups=mesh['member_0'=4,'member_1'=2,'member_2'=2,'tensor_0'=8,'tensor_1'=2] {..., dimensions={0} | all-to-all | bytes 442368 | tf_op jit(solution)/shard_map/all_to_all | solution.py:17
  81.4 5.1 %all-to-all-start.4 = ((bf16[16,128,320]{1,2,0:T(8,128)(2,1)}), bf16[16,128,320]{1,2,0:T(8,128)(2,1)S(1)}, u32[]{:S(2)}, u32[]{:S(2)}) async-start(bf16[16,128,320]{1,2,0:T(8,128)(2,1)} %broadcast_in_dim.49), calls=%async_computation.4 | async-start | bytes 2621440 | tf_op jit(solution)/shard_map/all_to_all | solution.py:17
  87.1 2.6 gather_fusion.1
  100.2 7.8 %all-to-all-done.4 = bf16[16,128,320]{1,2,0:T(8,128)(2,1)S(1)} async-done(((bf16[16,128,320]{1,2,0:T(8,128)(2,1)}), bf16[16,128,320]{1,2,0:T(8,128)(2,1)S(1)}, u32[]{:S(2)}, u32[]{:S(2)}) %all-to-all-start.4) | async-done | bytes 1310752 | tf_op jit(solution)/shard_map/all_to_all | solution.py:17
  109.9 3.9 %copy.181 = f32[8,1,128,864]{2,0,3,1:T(8,128)} copy(f32[8,1,128,864]{2,3,1,0:T(8,128)S(1)} %slice_multiply_fusion) | data formatting | bytes 7077888 | tf_op jit(solution)/shard_map/mul | solution.py:116
  114.1 3.9 %copy.174 = f32[8,1,128,864]{2,0,3,1:T(8,128)} copy(f32[8,1,128,864]{2,3,0,1:T(8,128)S(1)} %fusion.2) | data formatting | bytes 7077888 | tf_op jit(solution)/shard_map/mul | solution.py:115
  122.0 25.7 %convolution_convert_fusion = bf16[1024,5120]{1,0:T(8,128)(2,1)} fusion(bf16[864,5120]{0,1:T(8,128)(2,1)} %all-gather.2.cloned.1.call-done, f32[108,8,8,128]{3,2,1,0:T(8,128)} %bitcast.218, f32[108,8,8,128]{3,2,1,0:T(8,128)} %bitcast.220, f32[108,8,8,128]{3,2,1,0:T(8,128)} %bitcast.219, f32[108,8,8,128]{3,2,1,0:T(8,128)} %bitcast.221), kind=kOutput, calls=%fused_computation.2 | convolution fusion | flops 9072017408 | bytes 33488896 | tf_op jit(solution)/shard_map/dot_general | solution.py:123
  147.6 14.4 %copy.196 = bf16[1024,5120]{0,1:T(8,128)(2,1)} copy(bf16[1024,5120]{1,0:T(8,128)(2,1)} %convolution_convert_fusion) | data formatting | bytes 20971520
  163.3 8.5 %all-to-all-start.11 = ((bf16[8,1,8]{2,1,0:T(2,128)(2,1)}), bf16[8,1,8]{2,1,0:T(2,128)(2,1)S(1)}, u32[]{:S(2)}, u32[]{:S(2)}) async-start(bf16[8,1,8]{2,1,0:T(2,128)(2,1)} %broadcast_in_dim.98), calls=%async_computation.11 | async-start | bytes 8192 | tf_op jit(solution)/shard_map/all_to_all | solution.py:17
  172.8 5.2 %all-to-all-done.11 = bf16[8,1,8]{2,1,0:T(2,128)(2,1)S(1)} async-done(((bf16[8,1,8]{2,1,0:T(2,128)(2,1)}), bf16[8,1,8]{2,1,0:T(2,128)(2,1)S(1)}, u32[]{:S(2)}, u32[]{:S(2)}) %all-to-all-start.11) | async-done | bytes 160 | tf_op jit(solution)/shard_map/all_to_all | solution.py:17
  178.0 3.7 %all_to_all.78 = bf16[2,8,8]{2,1,0:T(8,128)(2,1)S(1)} all-to-all(bf16[2,8,8]{2,1,0:T(8,128)(2,1)S(1)} %broadcast_in_dim.100), channel_id=1, replica_groups=mesh['member_0'=4,'member_1'=2,'member_2'=2,'tensor_0'=8,'tensor_1'=2] {..., dimensions={0} | all-to-all | bytes 512 | tf_op jit(solution)/shard_map/all_to_all | solution.py:17
  181.7 5.0 %all-to-all-start.10 = ((bf16[16,8,3,4,320]{4,1,3,2,0:T(8,128)(2,1)}), bf16[16,8,3,4,320]{4,1,3,2,0:T(8,128)(2,1)S(1)}, u32[]{:S(2)}, u32[]{:S(2)}) async-start(bf16[16,8,3,4,320]{4,1,3,2,0:T(8,128)(2,1)} %copy-done.12), calls=%async_computation.10 | async-start | bytes 2359296 | tf_op jit(solution)/shard_map/all_to_all | solution.py:88
  186.7 17.2 %all-to-all-done.10 = bf16[16,8,3,4,320]{4,1,3,2,0:T(8,128)(2,1)S(1)} async-done(((bf16[16,8,3,4,320]{4,1,3,2,0:T(8,128)(2,1)}), bf16[16,8,3,4,320]{4,1,3,2,0:T(8,128)(2,1)S(1)}, u32[]{:S(2)}, u32[]{:S(2)}) %all-to-all-start.10) | async-done | bytes 983072 | tf_op jit(solution)/shard_map/all_to_all | solution.py:88
  205.4 5.8 %all-to-all-start.13 = ((bf16[8,8,3,4,864]{4,1,3,2,0:T(8,128)(2,1)}), bf16[8,8,3,4,864]{4,1,3,2,0:T(8,128)(2,1)S(1)}, u32[]{:S(2)}, u32[]{:S(2)}) async-start(bf16[8,8,3,4,864]{4,1,3,2,0:T(8,128)(2,1)} %broadcast_in_dim.101), calls=%async_computation.13 | async-start | bytes 2752512 | tf_op jit(solution)/shard_map/all_to_all | solution.py:17
  213.8 65.9 %reduce-scatter.7.cloned.1.call-done = bf16[640,1024]{1,0:T(8,128)(2,1)} async-done(((bf16[5120,1024]{1,0:T(8,128)(2,1)}), bf16[640,1024]{1,0:T(8,128)(2,1)}) %reduce-scatter.7.cloned.1.call-update) | async-done | bytes 1310736
  285.3 6.2 %all_to_all.79 = bf16[2,8,8,3,4,864]{5,2,1,4,3,0:T(8,128)(2,1)S(1)} all-to-all(bf16[2,8,8,3,4,864]{5,2,1,4,3,0:T(8,128)(2,1)S(1)} %broadcast_in_dim.102), channel_id=1, replica_groups=mesh['member_0'=4,'member_1'=2,'member_2'=2,'tensor_0'=8,'tensor_1'=2] {..., dimensions={0} | all-to-all | bytes 5308416 | tf_op jit(solution)/shard_map/all_to_all | solution.py:17
  297.4 5.5 %all-to-all-start.9 = ((f32[16,8,128,4]{2,1,3,0:T(8,128)}), f32[16,8,128,4]{2,1,3,0:T(8,128)S(1)}, u32[]{:S(2)}, u32[]{:S(2)}) async-start(f32[16,8,128,4]{2,1,3,0:T(8,128)} %broadcast_in_dim.54), calls=%async_computation.9 | async-start | bytes 524288 | tf_op jit(solution)/shard_map/all_to_all | solution.py:17
  302.9 2.6 fusion.15
  305.5 2.5 fusion.14
  308.0 7.1 %all-to-all-done.9 = f32[16,8,128,4]{2,1,3,0:T(8,128)S(1)} async-done(((f32[16,8,128,4]{2,1,3,0:T(8,128)}), f32[16,8,128,4]{2,1,3,0:T(8,128)S(1)}, u32[]{:S(2)}, u32[]{:S(2)}) %all-to-all-start.9) | async-done | bytes 262176 | tf_op jit(solution)/shard_map/all_to_all | solution.py:17
  315.2 2.3 fusion.13
  (132 shorter events, 45.5 us)
Async XLA Ops:
  7.2 61.5 %copy-start = (bf16[16,3,4,5120]{3,2,1,0:T(4,128)(2,1)S(1)}, bf16[16,3,4,5120]{3,2,1,0:T(4,128)(2,1)}, u32[]{:S(2)}) copy-start(bf16[16,3,4,5120]{3,2,1,0:T(4,128)(2,1)} %param.12) | copy-start | bytes 5898244
  7.2 6.8 %copy-start.15 = (bf16[128,320]{0,1:T(8,128)(2,1)S(1)}, bf16[128,320]{0,1:T(8,128)(2,1)}, u32[]{:S(2)}) copy-start(bf16[128,320]{0,1:T(8,128)(2,1)} %param.8) | copy-start | bytes 245764
  7.2 6.8 %copy-start.16 = (bf16[320,864]{1,0:T(8,128)(2,1)S(1)}, bf16[320,864]{1,0:T(8,128)(2,1)}, u32[]{:S(2)}) copy-start(bf16[320,864]{1,0:T(8,128)(2,1)} %param.9) | copy-start | bytes 1658884
  7.2 110.7 %all-gather.2.cloned.1.call-start = ((), (), s32[]{:S(2)}) async-start(), calls=%async_computation.17 | async-start | bytes 9748480 | tf_op jit(solution)/shard_map/all_gather | solution.py:125
  10.4 29.7 %copy-start.17 = (s32[8]{0:T(128)S(1)}, s32[8]{0:T(128)}, u32[]{:S(2)}) copy-start(s32[8]{0:T(128)} %param.14) | copy-start | bytes 100
  10.4 5.1 %all-to-all-start.5 = ((bf16[2,8,8,864]{3,2,1,0:T(8,128)(2,1)}), bf16[2,8,8,864]{3,2,1,0:T(8,128)(2,1)S(1)}, u32[]{:S(2)}, u32[]{:S(2)}) async-start(bf16[2,8,8,864]{3,2,1,0:T(8,128)(2,1)} %copy.176), calls=%async_computation.5 | async-start | bytes 458752 | tf_op jit(solution)/shard_map/all_to_all | solution.py:51
  15.5 5.0 %all-to-all-start = ((bf16[2,8,8,864]{3,2,1,0:T(8,128)(2,1)}), bf16[2,8,8,864]{3,2,1,0:T(8,128)(2,1)S(1)}, u32[]{:S(2)}, u32[]{:S(2)}) async-start(bf16[2,8,8,864]{3,2,1,0:T(8,128)(2,1)} %copy.167), calls=%async_computation | async-start | bytes 458752 | tf_op jit(solution)/shard_map/all_to_all | solution.py:51
  20.4 14.4 %all-to-all-start.6 = ((bf16[8,8,864]{2,1,0:T(8,128)(2,1)}), bf16[8,8,864]{2,1,0:T(8,128)(2,1)S(1)}, u32[]{:S(2)}, u32[]{:S(2)}) async-start(bf16[8,8,864]{2,1,0:T(8,128)(2,1)} %reduce_sum.77), calls=%async_computation.6 | async-start | bytes 229376 | tf_op jit(solution)/shard_map/all_to_all | solution.py:59
  34.9 11.6 %all-to-all-start.1 = ((bf16[8,8,864]{2,1,0:T(8,128)(2,1)}), bf16[8,8,864]{2,1,0:T(8,128)(2,1)S(1)}, u32[]{:S(2)}, u32[]{:S(2)}) async-start(bf16[8,8,864]{2,1,0:T(8,128)(2,1)} %reduce_sum.75), calls=%async_computation.1 | async-start | bytes 229376 | tf_op jit(solution)/shard_map/all_to_all | solution.py:59
  47.1 11.5 %all-to-all-start.7 = ((bf16[8,8,864]{2,1,0:T(8,128)(2,1)}), bf16[8,8,864]{2,1,0:T(8,128)(2,1)S(1)}, u32[]{:S(2)}, u32[]{:S(2)}) async-start(bf16[8,8,864]{2,1,0:T(8,128)(2,1)} %broadcast_in_dim.52), calls=%async_computation.7 | async-start | bytes 229376 | tf_op jit(solution)/shard_map/all_to_all | solution.py:17
  63.8 11.5 %all-to-all-start.2 = ((bf16[8,8,864]{2,1,0:T(8,128)(2,1)}), bf16[8,8,864]{2,1,0:T(8,128)(2,1)S(1)}, u32[]{:S(2)}, u32[]{:S(2)}) async-start(bf16[8,8,864]{2,1,0:T(8,128)(2,1)} %broadcast_in_dim.44), calls=%async_computation.2 | async-start | bytes 229376 | tf_op jit(solution)/shard_map/all_to_all | solution.py:17
  80.0 6.7 %copy-start.6 = (bf16[8,3,4,5120]{3,2,1,0:T(4,128)(2,1)S(1)}, bf16[8,3,4,5120]{3,2,1,0:T(4,128)(2,1)}, u32[]{:S(2)}) copy-start(bf16[8,3,4,5120]{3,2,1,0:T(4,128)(2,1)} %gather_fusion) | copy-start | bytes 2949124
  81.4 26.7 %all-to-all-start.4 = ((bf16[16,128,320]{1,2,0:T(8,128)(2,1)}), bf16[16,128,320]{1,2,0:T(8,128)(2,1)S(1)}, u32[]{:S(2)}, u32[]{:S(2)}) async-start(bf16[16,128,320]{1,2,0:T(8,128)(2,1)} %broadcast_in_dim.49), calls=%async_computation.4 | async-start | bytes 2621440 | tf_op jit(solution)/shard_map/all_to_all | solution.py:17
  86.5 193.2 %reduce-scatter.7.cloned.1.call-start = ((), (), s32[]{:S(2)}) async-start(), calls=%async_computation.18 | async-start | bytes 11796480
  87.1 99.6 %copy-start.3 = (bf16[8,3,4,5120]{3,0,2,1:T(8,128)(2,1)}, bf16[8,3,4,5120]{3,0,2,1:T(8,128)(2,1)S(1)}, u32[]{:S(2)}) copy-start(bf16[8,3,4,5120]{3,0,2,1:T(8,128)(2,1)S(1)} %copy_select_fusion) | copy-start | bytes 2949124
  89.6 4.0 %copy-start.14 = (bf16[2,8,8,864]{3,2,1,0:T(8,128)(2,1)S(1)}, bf16[2,8,8,864]{3,2,1,0:T(8,128)(2,1)}, u32[]{:S(2)}) copy-start(bf16[2,8,8,864]{3,2,1,0:T(8,128)(2,1)} %all_to_all.76) | copy-start | bytes 663556
  109.6 4.2 %copy-start.2 = (f32[8,2,128,864]{2,3,1,0:T(8,128)}, f32[8,2,128,864]{2,3,1,0:T(8,128)S(1)}, u32[]{:S(2)}) copy-start(f32[8,2,128,864]{2,3,1,0:T(8,128)S(1)} %fusion.18) | copy-start | bytes 21233668
  114.1 3.9 %copy-start.8 = (f32[128,864]{0,1:T(8,128)S(1)}, f32[128,864]{0,1:T(8,128)}, u32[]{:S(2)}) copy-start(f32[128,864]{0,1:T(8,128)} %copy.206) | copy-start | bytes 1327108
  163.3 14.7 %all-to-all-start.11 = ((bf16[8,1,8]{2,1,0:T(2,128)(2,1)}), bf16[8,1,8]{2,1,0:T(2,128)(2,1)S(1)}, u32[]{:S(2)}, u32[]{:S(2)}) async-start(bf16[8,1,8]{2,1,0:T(2,128)(2,1)} %broadcast_in_dim.98), calls=%async_computation.11 | async-start | bytes 8192 | tf_op jit(solution)/shard_map/all_to_all | solution.py:17
  172.8 5.2 %copy-start.12 = (bf16[16,8,3,4,320]{4,1,3,2,0:T(8,128)(2,1)}, bf16[16,8,3,4,320]{4,1,3,2,0:T(8,128)(2,1)S(1)}, u32[]{:S(2)}) copy-start(bf16[16,8,3,4,320]{4,1,3,2,0:T(8,128)(2,1)S(1)} %fusion.20) | copy-start | bytes 2949124
  181.7 22.3 %all-to-all-start.10 = ((bf16[16,8,3,4,320]{4,1,3,2,0:T(8,128)(2,1)}), bf16[16,8,3,4,320]{4,1,3,2,0:T(8,128)(2,1)S(1)}, u32[]{:S(2)}, u32[]{:S(2)}) async-start(bf16[16,8,3,4,320]{4,1,3,2,0:T(8,128)(2,1)} %copy-done.12), calls=%async_computation.10 | async-start | bytes 2359296 | tf_op jit(solution)/shard_map/all_to_all | solution.py:88
  186.7 24.4 %slice-start.2 = ((bf16[8,3,4,5120]{3,0,2,1:T(8,128)(2,1)}), bf16[8,1,4,5120]{3,0,2,1:T(8,128)(2,1)S(1)}, s32[]{:S(2)}) async-start(bf16[8,3,4,5120]{3,0,2,1:T(8,128)(2,1)} %copy-done.3), calls=%async_computation.22 | async-start | bytes 655360 | tf_op jit(solution)/shard_map/slice | solution.py:131
  205.4 79.3 %all-to-all-start.13 = ((bf16[8,8,3,4,864]{4,1,3,2,0:T(8,128)(2,1)}), bf16[8,8,3,4,864]{4,1,3,2,0:T(8,128)(2,1)S(1)}, u32[]{:S(2)}, u32[]{:S(2)}) async-start(bf16[8,8,3,4,864]{4,1,3,2,0:T(8,128)(2,1)} %broadcast_in_dim.101), calls=%async_computation.13 | async-start | bytes 2752512 | tf_op jit(solution)/shard_map/all_to_all | solution.py:17
  211.1 68.7 %copy-start.5 = (bf16[16,8,3,4,320]{4,1,3,2,0:T(8,128)(2,1)S(1)}, bf16[16,8,3,4,320]{4,1,3,2,0:T(8,128)(2,1)}, u32[]{:S(2)}) copy-start(bf16[16,8,3,4,320]{4,1,3,2,0:T(8,128)(2,1)} %copy-done.4) | copy-start | bytes 2949124
  211.1 104.1 %reduce-scatter.9.cloned.1.call-start = ((), (), s32[]{:S(2)}) async-start(), calls=%async_computation.19 | async-start | bytes 1966080
  285.3 9.3 %slice-start = ((s8[7077888]{0:T(1024)(128)(4,1)}), s8[4194304]{0:T(1024)(128)(4,1)S(1)}, s32[]{:S(2)}) async-start(s8[7077888]{0:T(1024)(128)(4,1)} %bitcast.214), calls=%async_computation.20 | async-start | bytes 8388608
  291.5 3.4 %slice-start.1 = ((s8[7077888]{0:T(1024)(128)(4,1)}), s8[2883584]{0:T(1024)(128)(4,1)S(1)}, s32[]{:S(2)}) async-start(s8[7077888]{0:T(1024)(128)(4,1)} %bitcast.214), calls=%async_computation.21 | async-start | bytes 5767168
  291.8 4.9 %copy-start.7 = (bf16[8,2,8,3,4,864]{5,2,1,0,4,3:T(8,128)(2,1)}, bf16[8,2,8,3,4,864]{5,2,1,0,4,3:T(8,128)(2,1)S(1)}, u32[]{:S(2)}) copy-start(bf16[8,2,8,3,4,864]{5,2,1,0,4,3:T(8,128)(2,1)S(1)} %copy.192) | copy-start | bytes 7962628
  291.8 3.3 %copy-start.9 = (f32[128,864]{0,1:T(8,128)S(1)}, f32[128,864]{0,1:T(8,128)}, u32[]{:S(2)}) copy-start(f32[128,864]{0,1:T(8,128)} %copy.206) | copy-start | bytes 1327108
  291.8 3.4 %copy-start.11 = (f32[128,864]{0,1:T(8,128)S(1)}, f32[128,864]{0,1:T(8,128)}, u32[]{:S(2)}) copy-start(f32[128,864]{0,1:T(8,128)} %copy.205) | copy-start | bytes 1327108
  297.4 17.7 %all-to-all-start.9 = ((f32[16,8,128,4]{2,1,3,0:T(8,128)}), f32[16,8,128,4]{2,1,3,0:T(8,128)S(1)}, u32[]{:S(2)}, u32[]{:S(2)}) async-start(f32[16,8,128,4]{2,1,3,0:T(8,128)} %broadcast_in_dim.54), calls=%async_computation.9 | async-start | bytes 524288 | tf_op jit(solution)/shard_map/all_to_all | solution.py:17
  302.9 14.7 %copy-start.1 = (bf16[16,3,4,5120]{3,2,1,0:T(4,128)(2,1)S(1)}, bf16[16,3,4,5120]{3,2,1,0:T(4,128)(2,1)}, u32[]{:S(2)}) copy-start(bf16[16,3,4,5120]{3,2,1,0:T(4,128)(2,1)} %param.12) | copy-start | bytes 5898244
  (4 other events, 5.8 us)
Sparse Core Ops, SparseCore 0:
  10.7 97.9 all-gather.1
  162.2 117.4 reduce-scatter.6
  282.2 27.6 reduce-scatter.8
